TPU v7x, 32 devices: a whole 2x2x4 slice. The times are simulated.
32 devices in a mesh: freq: 2 (over x), panel: 16 (over z, y, core).
Axes of the slice: x: 2, y: 2, z: 4, core: 2. Of those that a mesh axis runs over, the one named last changes fastest.
Arguments:
- recorded: float32 [2, 2, 2048, 2048], P('freq', None, 'panel'), parts along dimension 0, may hold values from -60 to 60
- receiver_kernel: bfloat16 [2, 2, 4095], P('freq'), parts along dimension 0, may hold values from -1.5 to 1.5
- source_kernel: bfloat16 [2, 2, 4095], P('freq'), parts along dimension 0, may hold values from -1.5 to 1.5
Outputs:
- primaries: float32 [2, 2, 2048, 2048], P('freq', None, 'panel'), parts along dimension 0
- multiples: bfloat16 [2, 2, 2048, 2048], P('freq', None, 'panel'), parts along dimension 0
There are 2 independent parts, one for each index of `freq`. A program takes and returns all parts, laid end to end along the dimension named above; each array names one. Nothing has to cross between parts.
All inputs are finite; a program needn't handle non-finite values.
Results may differ from a plain program's by a relative error of at most 0.0057.
Values may be sent and summed in bfloat16 or wider, within the bound.
A program may use at most 320 MiB of HBM per device.

v0:
```python
import functools

import jax
import jax.numpy as jnp
from jax import lax
from jax.experimental import pallas as pl
from jax.experimental.pallas import tpu as pltpu
from jax.sharding import PartitionSpec as P

MESH = pl.DeviceIdType.MESH
LANES = 128
GROUP = 256
STRIP = 16
STRIPS = 4


def spread(taps_ref, padded, comp, flipped):
    length = padded.shape[1]
    rows = [padded[comp : comp + 1, at : at + LANES] for at in range(0, length, LANES)]
    if not flipped:
        return jnp.broadcast_to(jnp.concatenate(rows, axis=1), (STRIP, length))
    i = lax.broadcasted_iota(jnp.int32, (LANES, LANES), 0)
    j = lax.broadcasted_iota(jnp.int32, (LANES, LANES), 1)
    swap = jnp.where(i + j == LANES - 1, 1.0, 0.0).astype(jnp.bfloat16)
    tall = jnp.concatenate([jnp.broadcast_to(r, (STRIP, LANES)) for r in rows[::-1]], axis=0)
    tall = jnp.dot(tall.astype(jnp.bfloat16), swap, preferred_element_type=jnp.float32)
    return jnp.concatenate([tall[at : at + STRIP] for at in range(0, tall.shape[0], STRIP)], axis=1)


def skew(taps_ref, padded, flipped, block, band_ref):
    length = padded.shape[1]
    padded[...] = jnp.zeros_like(padded)
    padded[:, 0 : length - 1] = taps_ref[0].astype(jnp.float32)
    row = lax.broadcasted_iota(jnp.int32, (STRIP, length), 0)
    for comp in range(2):
        x = spread(taps_ref, padded, comp, flipped)
        step = 1
        while step < STRIP:
            x = jnp.where((row & step) != 0, pltpu.roll(x, step, 1), x)
            step *= 2
        lane0 = comp * block
        for s in range(0, LANES, STRIP):
            shift = (s - (LANES - block) + (0 if flipped else 1)) % length
            y = (pltpu.roll(x, shift, 1) if shift else x).astype(jnp.bfloat16)
            for m in range(length // LANES):
                at = length - LANES * (m + 1)
                band_ref[m * LANES + s : m * LANES + s + STRIP, lane0 : lane0 + block] = y[:, at : at + block]


def exchange_kernel(
    panels,
    rec_hbm,
    rtaps_hbm,
    staps_hbm,
    rec_ref,
    mult_ref,
    fit_ref,
    rtaps_ref,
    staps_ref,
    load_sem,
    padded,
    band_r,
    band_s,
    w1,
    w2,
    foc,
    foc_in,
    mul,
    mul_in,
    sums,
    sums_in,
    send1,
    recv1,
    send2,
    recv2,
    send3,
    recv3,
):
    me = lax.axis_index("panel")
    rows, width = rec_ref.shape[2], rec_ref.shape[3]
    sources = rows * panels
    cols = width // panels
    halves, hc = foc_in.shape[0], foc_in.shape[2]
    nt = (((1,), (1,)), ((), ()))

    def order(n, own, groups):
        side = groups // 2
        half = lax.rem(own // side + 1 + n // side, 2)
        return half * side + lax.rem(own + 1 + n, side)

    def peer(o):
        return lax.rem(me + o, panels)

    loads = [
        pltpu.make_async_copy(src, dst, load_sem.at[i])
        for i, (src, dst) in enumerate(
            ((rtaps_hbm, rtaps_ref), (rec_hbm, rec_ref), (staps_hbm, staps_ref))
        )
    ]
    for load in loads:
        load.start()

    barrier = pltpu.get_barrier_semaphore()

    @pl.loop(1, panels)
    def _(o):
        pl.semaphore_signal(barrier, inc=1, device_id={"panel": peer(o)}, device_id_type=MESH)

    loads[0].wait()
    skew(rtaps_ref, padded, True, LANES, band_r)
    loads[1].wait()
    for kb in range(width // LANES):
        re = rec_ref[0, 0, :, kb * LANES : (kb + 1) * LANES].astype(jnp.bfloat16)
        im = rec_ref[0, 1, :, kb * LANES : (kb + 1) * LANES].astype(jnp.bfloat16)
        at = 2 * kb * LANES
        w1[0:rows, at : at + LANES] = re
        w1[0:rows, at + LANES : at + 2 * LANES] = -im
        w1[rows : 2 * rows, at : at + LANES] = im
        w1[rows : 2 * rows, at + LANES : at + 2 * LANES] = re

    pl.semaphore_wait(barrier, panels - 1)

    def copy1(h, dest, src):
        return pltpu.make_async_remote_copy(
            src_ref=foc.at[pl.ds(pl.multiple_of(dest * cols + h * hc, hc), hc), :],
            dst_ref=foc_in.at[h, src],
            send_sem=send1.at[h, dest],
            recv_sem=recv1.at[h, src],
            device_id={"panel": dest},
            device_id_type=MESH,
        )

    def copy2(h, dest, src):
        return pltpu.make_async_remote_copy(
            src_ref=mul.at[h, pl.ds(pl.multiple_of(dest * rows, rows), rows), :],
            dst_ref=mul_in.at[h, src],
            send_sem=send2.at[h, dest],
            recv_sem=recv2.at[h, src],
            device_id={"panel": dest},
            device_id_type=MESH,
        )

    def copy3(dest, src):
        return pltpu.make_async_remote_copy(
            src_ref=sums,
            dst_ref=sums_in.at[src],
            send_sem=send3.at[dest],
            recv_sem=recv3.at[src],
            device_id={"panel": dest},
            device_id_type=MESH,
        )

    groups1 = width // GROUP
    per1 = GROUP // cols
    own1 = me // per1

    @pl.loop(0, groups1)
    def _(n):
        g = order(n, own1, groups1)
        first = pl.multiple_of(g * GROUP, GROUP)
        lhs = jnp.concatenate(
            [
                band_r[pl.ds(pl.multiple_of(width - LANES * (kb + 1) + first, LANES), GROUP), :]
                for kb in range(width // LANES)
            ],
            axis=1,
        )
        out = lax.dot_general(lhs, w1[...], nt, preferred_element_type=jnp.float32)
        foc[pl.ds(first, GROUP), :] = out.astype(jnp.bfloat16)
        for d in range(per1):
            dest = g * per1 + d

            @pl.when(dest != me)
            def _():
                copy1(0, dest, me).start()

    for h in range(1, halves):

        @pl.loop(0, groups1)
        def _(n):
            for d in range(per1):
                dest = order(n, own1, groups1) * per1 + d

                @pl.when(dest != me)
                def _():
                    copy1(h, dest, me).start()

    for h in range(halves):
        foc_in[h, me] = foc[pl.ds(pl.multiple_of(me * cols + h * hc, hc), hc), :]
    loads[2].wait()
    skew(staps_ref, padded, False, rows, band_s)

    groups2 = sources // GROUP
    per2 = GROUP // rows
    own2 = me // per2
    lane = lax.broadcasted_iota(jnp.int32, (hc, 2 * rows), 1)
    for h in range(halves):

        @pl.loop(1, panels)
        def _(o):
            copy1(h, peer(o), peer(o)).wait_recv()

        for j in range(panels):
            x = foc_in[h, j]
            at = 2 * rows * j
            w2[0:hc, at : at + 2 * rows] = jnp.where(lane < rows, x, -x)
            w2[hc : 2 * hc, at : at + 2 * rows] = jnp.concatenate([x[:, rows:], x[:, :rows]], axis=1)

        @pl.loop(0, groups2)
        def _(n):
            g = order(n, own2, groups2)
            first = pl.multiple_of(g * GROUP, GROUP)
            lhs = jnp.concatenate(
                [
                    band_s[pl.ds(pl.multiple_of(sources - rows * (jb + 1) + first, rows), GROUP), :]
                    for jb in range(panels)
                ],
                axis=1,
            )
            out = lax.dot_general(lhs, w2[...], nt, preferred_element_type=jnp.float32)
            mul[h, pl.ds(first, GROUP), :] = out.astype(jnp.bfloat16)
            for d in range(per2):
                dest = g * per2 + d

                @pl.when(dest != me)
                def _():
                    copy2(h, dest, me).start()

        mul_in[h, me] = mul[h, pl.ds(pl.multiple_of(me * rows, rows), rows), :]

    def fold(v):
        return jnp.sum(v, axis=0, keepdims=True)

    chunks = width // LANES
    near = LANES // cols

    def gather(n, acc):
        cb = order(n, me // near, chunks)
        blocks = []
        for d in range(near):
            src = cb * near + d

            @pl.when(src != me)
            def _():
                for h in range(halves):
                    copy2(h, src, src).wait_recv()

            blocks += [mul_in[h, src] for h in range(halves)]
        mre = jnp.concatenate([b[:, :hc] for b in blocks], axis=1)
        mim = jnp.concatenate([b[:, hc:] for b in blocks], axis=1)
        at = pl.ds(pl.multiple_of(cb * LANES, LANES), LANES)
        mult_ref[0, 0, :, at] = mre
        mult_ref[0, 1, :, at] = mim
        mre = mre.astype(jnp.float32)
        mim = mim.astype(jnp.float32)
        pre = rec_ref[0, 0, :, at]
        pim = rec_ref[0, 1, :, at]
        return (
            acc[0] + fold(mre * pre + mim * pim),
            acc[1] + fold(mre * pim - mim * pre),
            acc[2] + fold(mre * mre + mim * mim),
        )

    zero = jnp.zeros((1, LANES), jnp.float32)
    num_re, num_im, energy = lax.fori_loop(0, chunks, gather, (zero, zero, zero))
    part = jnp.concatenate([num_re, num_im, energy, jnp.zeros((5, LANES), jnp.float32)], axis=0)
    sums[...] = part
    sums_in[me] = part

    @pl.loop(1, panels)
    def _(o):
        copy3(peer(o), me).start()

    @pl.loop(1, panels)
    def _(o):
        for h in range(halves):
            copy1(h, peer(o), me).wait_send()
            copy2(h, peer(o), me).wait_send()

    @pl.loop(1, panels)
    def _(o):
        copy3(peer(o), peer(o)).wait_recv()

    @pl.loop(1, panels)
    def _(o):
        copy3(peer(o), me).wait_send()

    total = jnp.sum(jnp.sum(sums_in[...], axis=0), axis=1, keepdims=True)
    fit = total[0:2, :] / (total[2:3, :] + 1e-06)
    fit_ref[...] = jnp.broadcast_to(
        jnp.concatenate([fit, jnp.zeros((6, 1), jnp.float32)], axis=0), (8, LANES)
    )


def subtract_kernel(rec_ref, mult_ref, fit_ref, prim_hbm, mult_hbm, prim, sem):
    mult_out = pltpu.make_async_copy(mult_ref, mult_hbm, sem.at[0])
    mult_out.start()
    fit_re = fit_ref[0:1, 0:1]
    fit_im = fit_ref[1:2, 0:1]
    rows = rec_ref.shape[2]
    strip = rows // STRIPS
    outs = []
    for i in range(STRIPS):
        at = slice(i * strip, (i + 1) * strip)
        mre = mult_ref[0, 0, at, :].astype(jnp.float32)
        mim = mult_ref[0, 1, at, :].astype(jnp.float32)
        prim[0, 0, at, :] = rec_ref[0, 0, at, :] - (fit_re * mre - fit_im * mim)
        prim[0, 1, at, :] = rec_ref[0, 1, at, :] - (fit_re * mim + fit_im * mre)
        out = pltpu.make_async_copy(prim.at[:, :, at, :], prim_hbm.at[:, :, at, :], sem.at[i + 1])
        out.start()
        outs.append(out)
    for out in outs:
        out.wait()
    mult_out.wait()


def per_device(recorded, receiver_kernel, source_kernel):
    rows, width = recorded.shape[2], recorded.shape[3]
    panels = lax.axis_size("panel")
    sources = rows * panels
    cols = width // panels
    bf16 = jnp.bfloat16
    vmem = pl.BlockSpec(memory_space=pltpu.VMEM)
    hc = min(cols, LANES // 2)
    halves = cols // hc
    sem = pltpu.SemaphoreType.DMA((panels,))
    sems = pltpu.SemaphoreType.DMA((halves, panels))
    hbm = pl.BlockSpec(memory_space=pltpu.HBM)
    rec, mult, fit = pl.pallas_call(
        functools.partial(exchange_kernel, panels),
        out_shape=(
            jax.ShapeDtypeStruct(recorded.shape, jnp.float32),
            jax.ShapeDtypeStruct(recorded.shape, bf16),
            jax.ShapeDtypeStruct((8, LANES), jnp.float32),
        ),
        in_specs=[hbm] * 3,
        out_specs=(vmem, vmem, vmem),
        scratch_shapes=[
            pltpu.VMEM(receiver_kernel.shape, bf16),
            pltpu.VMEM(source_kernel.shape, bf16),
            pltpu.SemaphoreType.DMA((3,)),
            pltpu.VMEM((2, 2 * width), jnp.float32),
            pltpu.VMEM((2 * width, 2 * LANES), bf16),
            pltpu.VMEM((2 * sources, 2 * rows), bf16),
            pltpu.VMEM((2 * rows, 2 * width), bf16),
            pltpu.VMEM((2 * hc, 2 * sources), bf16),
            pltpu.VMEM((width, 2 * rows), bf16),
            pltpu.VMEM((halves, panels, hc, 2 * rows), bf16),
            pltpu.VMEM((halves, sources, 2 * hc), bf16),
            pltpu.VMEM((halves, panels, rows, 2 * hc), bf16),
            pltpu.VMEM((8, LANES), jnp.float32),
            pltpu.VMEM((panels, 8, LANES), jnp.float32),
            sems,
            sems,
            sems,
            sems,
            sem,
            sem,
        ],
        compiler_params=pltpu.CompilerParams(collective_id=0, has_side_effects=True, vmem_limit_bytes=50 * 2**20),
        name="exchange",
    )(
        *(pltpu.with_memory_space_constraint(x, pltpu.HBM) for x in (recorded, receiver_kernel, source_kernel))
    )
    return pl.pallas_call(
        subtract_kernel,
        out_shape=(
            jax.ShapeDtypeStruct(recorded.shape, jnp.float32),
            jax.ShapeDtypeStruct(recorded.shape, bf16),
        ),
        in_specs=[vmem] * 3,
        out_specs=(hbm, hbm),
        scratch_shapes=[pltpu.VMEM(recorded.shape, jnp.float32), pltpu.SemaphoreType.DMA((STRIPS + 1,))],
        compiler_params=pltpu.CompilerParams(vmem_limit_bytes=12 * 2**20),
        name="subtract",
    )(rec, mult, fit)


def solution(mesh):
    placed = (P("freq", None, "panel", None), P("freq", None, None), P("freq", None, None))
    return jax.shard_map(
        per_device,
        mesh=mesh,
        in_specs=placed,
        out_specs=(P("freq", None, "panel", None), P("freq", None, "panel", None)),
        check_vma=False,
    )
```

profile of v0, /device:TPU:0, one launch (start us, length us, event | category | flops | bytes accessed | tf_op | source)
XLA Modules:
  0.0 62.3 jit_solution(2097953449456151773)
XLA Ops:
  0.6 60.0 %exchange.1 = (f32[1,2,128,2048]{3,2,1,0:T(8,128)S(1)}, bf16[1,2,128,2048]{3,2,1,0:T(8,128)(2,1)S(1)}, f32[8,128]{1,0:T(8,128)S(1)}) custom-call(f32[1,2,128,2048]{3,2,1,0:T(8,128)} %rec_hbm.1, bf16[1,2,4095]{2,1,0:T(2,128)(2,1)} %rtaps_hbm.1, bf16[1,2,4095]{2,1,0:T(2,128)(2,1)} %staps_hbm.1), custom_call_target="tpu_custom_call" | custom-call | tf_op jit(solution)/shard_map/exchange/pallas_call | solution.py:329
  60.6 1.7 %subtract.1 = (f32[1,2,128,2048]{3,2,1,0:T(8,128)}, bf16[1,2,128,2048]{3,2,1,0:T(8,128)(2,1)}) custom-call(f32[1,2,128,2048]{3,2,1,0:T(8,128)S(1)} %get-tuple-element.5.rec_ref, bf16[1,2,128,2048]{3,2,1,0:T(8,128)(2,1)S(1)} %get-tuple-element.6.mult_ref, f32[8,128]{1,0:T(8,128)S(1)} %get-tuple-element.7.fit_ref), custom_call_target="tpu_custom_call" | custom-call | tf_op jit(solution)/shard_map/subtract/pallas_call | solution.py:365
where the time goes:
time: 62.6 us; the launch traced here: 62.3 us
  Pallas kernels  61.7 us (99%)
  between operations  0.64 us (1%)
    pallas_call x1, Pallas kernels, per_device(): pl.pallas_call(functools.partial(exchange_kernel, panels), out_shape=(jax...  60 us
    pallas_call x1, Pallas kernels, per_device(): pl.pallas_call(subtract_kernel, out_shape=(jax.ShapeDtypeStruct(recorded....  1.7 us

commit v1 on v0

--- a/solution.py
+++ b/solution.py
@@ -12,6 +12,7 @@
 GROUP = 256
 STRIP = 16
 STRIPS = 4
+PLANES = 4
 
 
 def spread(taps_ref, padded, comp, flipped):
@@ -82,11 +83,14 @@
     cols = width // panels
     halves, hc = foc_in.shape[0], foc_in.shape[2]
     nt = (((1,), (1,)), ((), ()))
+    planes = recv2.shape[0]
+    side = panels // planes
+    plane = me // side
 
     def order(n, own, groups):
-        side = groups // 2
-        half = lax.rem(own // side + 1 + n // side, 2)
-        return half * side + lax.rem(own + 1 + n, side)
+        half = groups // 2
+        far = lax.rem(own // half + 1 + n // half, 2)
+        return far * half + lax.rem(own + 1 + n, half)
 
     def peer(o):
         return lax.rem(me + o, panels)
@@ -124,8 +128,8 @@
         return pltpu.make_async_remote_copy(
             src_ref=foc.at[pl.ds(pl.multiple_of(dest * cols + h * hc, hc), hc), :],
             dst_ref=foc_in.at[h, src],
-            send_sem=send1.at[h, dest],
-            recv_sem=recv1.at[h, src],
+            send_sem=send1,
+            recv_sem=recv1.at[h],
             device_id={"panel": dest},
             device_id_type=MESH,
         )
@@ -134,18 +138,21 @@
         return pltpu.make_async_remote_copy(
             src_ref=mul.at[h, pl.ds(pl.multiple_of(dest * rows, rows), rows), :],
             dst_ref=mul_in.at[h, src],
-            send_sem=send2.at[h, dest],
-            recv_sem=recv2.at[h, src],
+            send_sem=send2,
+            recv_sem=recv2.at[src // side],
             device_id={"panel": dest},
             device_id_type=MESH,
         )
+
+    def drain(ref, sem):
+        pltpu.make_async_copy(ref, ref, sem).wait()
 
     def copy3(dest, src):
         return pltpu.make_async_remote_copy(
             src_ref=sums,
             dst_ref=sums_in.at[src],
-            send_sem=send3.at[dest],
-            recv_sem=recv3.at[src],
+            send_sem=send3,
+            recv_sem=recv3,
             device_id={"panel": dest},
             device_id_type=MESH,
         )
@@ -195,11 +202,7 @@
     own2 = me // per2
     lane = lax.broadcasted_iota(jnp.int32, (hc, 2 * rows), 1)
     for h in range(halves):
-
-        @pl.loop(1, panels)
-        def _(o):
-            copy1(h, peer(o), peer(o)).wait_recv()
-
+        drain(foc_in.at[h, pl.ds(0, panels - 1)], recv1.at[h])
         for j in range(panels):
             x = foc_in[h, j]
             at = 2 * rows * j
@@ -231,38 +234,42 @@
     def fold(v):
         return jnp.sum(v, axis=0, keepdims=True)
 
-    chunks = width // LANES
     near = LANES // cols
-
-    def gather(n, acc):
-        cb = order(n, me // near, chunks)
-        blocks = []
-        for d in range(near):
-            src = cb * near + d
-
-            @pl.when(src != me)
-            def _():
-                for h in range(halves):
-                    copy2(h, src, src).wait_recv()
-
-            blocks += [mul_in[h, src] for h in range(halves)]
-        mre = jnp.concatenate([b[:, :hc] for b in blocks], axis=1)
-        mim = jnp.concatenate([b[:, hc:] for b in blocks], axis=1)
-        at = pl.ds(pl.multiple_of(cb * LANES, LANES), LANES)
-        mult_ref[0, 0, :, at] = mre
-        mult_ref[0, 1, :, at] = mim
-        mre = mre.astype(jnp.float32)
-        mim = mim.astype(jnp.float32)
-        pre = rec_ref[0, 0, :, at]
-        pim = rec_ref[0, 1, :, at]
-        return (
-            acc[0] + fold(mre * pre + mim * pim),
-            acc[1] + fold(mre * pim - mim * pre),
-            acc[2] + fold(mre * mre + mim * mim),
-        )
+    chunks = side // near
+
+    def gather(q, count, acc):
+        if count:
+            drain(mul_in.at[:, pl.ds(q * side, count)], recv2.at[q])
+
+        def step(n, acc):
+            cb = q * chunks + n
+            blocks = [mul_in[h, cb * near + d] for d in range(near) for h in range(halves)]
+            mre = jnp.concatenate([b[:, :hc] for b in blocks], axis=1)
+            mim = jnp.concatenate([b[:, hc:] for b in blocks], axis=1)
+            at = pl.ds(pl.multiple_of(cb * LANES, LANES), LANES)
+            mult_ref[0, 0, :, at] = mre
+            mult_ref[0, 1, :, at] = mim
+            mre = mre.astype(jnp.float32)
+            mim = mim.astype(jnp.float32)
+            pre = rec_ref[0, 0, :, at]
+            pim = rec_ref[0, 1, :, at]
+            return (
+                acc[0] + fold(mre * pre + mim * pim),
+                acc[1] + fold(mre * pim - mim * pre),
+                acc[2] + fold(mre * mre + mim * mim),
+            )
+
+        return lax.fori_loop(0, chunks, step, acc)
 
     zero = jnp.zeros((1, LANES), jnp.float32)
-    num_re, num_im, energy = lax.fori_loop(0, chunks, gather, (zero, zero, zero))
+    sides = gather(plane, side - 1, (zero, zero, zero))
+
+    def visit(n, acc):
+        p = jnp.where(plane < planes // 2, plane, planes - 1 - plane)
+        q = jnp.where(n < planes // 2 - 1, n + (n >= p), planes + planes // 2 - 2 - n)
+        return gather(jnp.where(plane < planes // 2, q, planes - 1 - q), side, acc)
+
+    num_re, num_im, energy = lax.fori_loop(0, planes - 1, visit, sides)
     part = jnp.concatenate([num_re, num_im, energy, jnp.zeros((5, LANES), jnp.float32)], axis=0)
     sums[...] = part
     sums_in[me] = part
@@ -271,19 +278,10 @@
     def _(o):
         copy3(peer(o), me).start()
 
-    @pl.loop(1, panels)
-    def _(o):
-        for h in range(halves):
-            copy1(h, peer(o), me).wait_send()
-            copy2(h, peer(o), me).wait_send()
-
-    @pl.loop(1, panels)
-    def _(o):
-        copy3(peer(o), peer(o)).wait_recv()
-
-    @pl.loop(1, panels)
-    def _(o):
-        copy3(peer(o), me).wait_send()
+    drain(foc.at[pl.ds(0, width - cols), :], send1)
+    drain(mul.at[:, pl.ds(0, sources - rows), :], send2)
+    drain(sums_in.at[pl.ds(0, panels - 1)], recv3)
+    drain(sums_in.at[pl.ds(0, panels - 1)], send3)
 
     total = jnp.sum(jnp.sum(sums_in[...], axis=0), axis=1, keepdims=True)
     fit = total[0:2, :] / (total[2:3, :] + 1e-06)
@@ -323,8 +321,8 @@
     vmem = pl.BlockSpec(memory_space=pltpu.VMEM)
     hc = min(cols, LANES // 2)
     halves = cols // hc
-    sem = pltpu.SemaphoreType.DMA((panels,))
-    sems = pltpu.SemaphoreType.DMA((halves, panels))
+    planes = PLANES if panels % PLANES == 0 else 1
+    sem = pltpu.SemaphoreType.DMA
     hbm = pl.BlockSpec(memory_space=pltpu.HBM)
     rec, mult, fit = pl.pallas_call(
         functools.partial(exchange_kernel, panels),
@@ -338,7 +336,7 @@
         scratch_shapes=[
             pltpu.VMEM(receiver_kernel.shape, bf16),
             pltpu.VMEM(source_kernel.shape, bf16),
-            pltpu.SemaphoreType.DMA((3,)),
+            sem((3,)),
             pltpu.VMEM((2, 2 * width), jnp.float32),
             pltpu.VMEM((2 * width, 2 * LANES), bf16),
             pltpu.VMEM((2 * sources, 2 * rows), bf16),
@@ -350,10 +348,10 @@
             pltpu.VMEM((halves, panels, rows, 2 * hc), bf16),
             pltpu.VMEM((8, LANES), jnp.float32),
             pltpu.VMEM((panels, 8, LANES), jnp.float32),
-            sems,
-            sems,
-            sems,
-            sems,
+            sem,
+            sem((halves,)),
+            sem,
+            sem((planes,)),
             sem,
             sem,
         ],

time: 62.6 us -> 60.8 us (0.971)
  Pallas kernels: 61.7 us -> 59.9 us
    pallas_call x1, Pallas kernels: 60 us -> 58.2 us  [per_device(): pl.pallas_call(functools.partial(exchange_kernel, panels), out_shape=(jax...]
where the time goes in v1:
time: 60.8 us; the launch traced here: 60.6 us
  Pallas kernels  59.9 us (99%)
  between operations  0.64 us (1%)
    pallas_call x1, Pallas kernels, per_device(): pl.pallas_call(functools.partial(exchange_kernel, panels), out_shape=(jax...  58.2 us
    pallas_call x1, Pallas kernels, per_device(): pl.pallas_call(subtract_kernel, out_shape=(jax.ShapeDtypeStruct(recorded....  1.7 us

profile of v1, /device:TPU:0, one launch (start us, length us, event | category | flops | bytes accessed | tf_op | source)
XLA Modules:
  0.0 60.6 jit_solution(17483774922097630798)
XLA Ops:
  0.6 58.2 %exchange.1 = (f32[1,2,128,2048]{3,2,1,0:T(8,128)S(1)}, bf16[1,2,128,2048]{3,2,1,0:T(8,128)(2,1)S(1)}, f32[8,128]{1,0:T(8,128)S(1)}) custom-call(f32[1,2,128,2048]{3,2,1,0:T(8,128)} %rec_hbm.1, bf16[1,2,4095]{2,1,0:T(2,128)(2,1)} %rtaps_hbm.1, bf16[1,2,4095]{2,1,0:T(2,128)(2,1)} %staps_hbm.1), custom_call_target="tpu_custom_call" | custom-call | tf_op jit(solution)/shard_map/exchange/pallas_call | solution.py:327
  58.9 1.7 %subtract.1 = (f32[1,2,128,2048]{3,2,1,0:T(8,128)}, bf16[1,2,128,2048]{3,2,1,0:T(8,128)(2,1)}) custom-call(f32[1,2,128,2048]{3,2,1,0:T(8,128)S(1)} %get-tuple-element.5.rec_ref, bf16[1,2,128,2048]{3,2,1,0:T(8,128)(2,1)S(1)} %get-tuple-element.6.mult_ref, f32[8,128]{1,0:T(8,128)S(1)} %get-tuple-element.7.fit_ref), custom_call_target="tpu_custom_call" | custom-call | tf_op jit(solution)/shard_map/subtract/pallas_call | solution.py:363

commit v2 on v1

--- a/solution.py
+++ b/solution.py
@@ -76,6 +76,7 @@
     recv2,
     send3,
     recv3,
+    relay,
 ):
     me = lax.axis_index("panel")
     rows, width = rec_ref.shape[2], rec_ref.shape[3]
@@ -87,10 +88,12 @@
     side = panels // planes
     plane = me // side
 
-    def order(n, own, groups):
+    def order(n, own, groups, rev=0):
         half = groups // 2
         far = lax.rem(own // half + 1 + n // half, 2)
-        return far * half + lax.rem(own + 1 + n, half)
+        at = lax.rem(n, half)
+        at = jnp.where(far == 1 - rev, half - 1 - at, at)
+        return far * half + at + jnp.where(lax.rem(at, 2) == 0, 1, -1) * lax.rem(own, 2)
 
     def peer(o):
         return lax.rem(me + o, panels)
@@ -106,9 +109,24 @@
 
     barrier = pltpu.get_barrier_semaphore()
 
-    @pl.loop(1, panels)
+    @pl.loop(0, panels)
     def _(o):
-        pl.semaphore_signal(barrier, inc=1, device_id={"panel": peer(o)}, device_id_type=MESH)
+        gap = jnp.abs(o // side - plane)
+
+        @pl.when(jnp.logical_and(gap <= 1, o != me))
+        def _():
+            pl.semaphore_signal(barrier, inc=1, device_id={"panel": o}, device_id_type=MESH)
+
+    above = (plane > 0).astype(jnp.int32)
+    below = (plane < planes - 1).astype(jnp.int32)
+
+    outer = jnp.logical_or(plane == 0, plane == planes - 1)
+    inner = jnp.logical_not(outer)
+    outward = jnp.where(plane * 2 < planes, -side, side)
+    inward = -outward
+
+    def tell(slot, step):
+        pl.semaphore_signal(relay.at[slot], inc=1, device_id={"panel": me + step}, device_id_type=MESH)
 
     loads[0].wait()
     skew(rtaps_ref, padded, True, LANES, band_r)
@@ -122,7 +140,13 @@
         w1[rows : 2 * rows, at : at + LANES] = im
         w1[rows : 2 * rows, at + LANES : at + 2 * LANES] = re
 
-    pl.semaphore_wait(barrier, panels - 1)
+    pl.semaphore_wait(barrier, side * (1 + above + below) - 1)
+    if planes > 1:
+
+        @pl.when(inner)
+        def _():
+            tell(0, inward)
+            tell(1, outward)
 
     def copy1(h, dest, src):
         return pltpu.make_async_remote_copy(
@@ -163,7 +187,14 @@
 
     @pl.loop(0, groups1)
     def _(n):
-        g = order(n, own1, groups1)
+        g = order(n, own1, groups1, 1)
+        if planes > 1:
+
+            @pl.when(jnp.logical_and(inner, n == groups1 // planes))
+            def _():
+                pl.semaphore_wait(relay.at[0], 1)
+                tell(2, outward)
+
         first = pl.multiple_of(g * GROUP, GROUP)
         lhs = jnp.concatenate(
             [
@@ -174,6 +205,16 @@
         )
         out = lax.dot_general(lhs, w1[...], nt, preferred_element_type=jnp.float32)
         foc[pl.ds(first, GROUP), :] = out.astype(jnp.bfloat16)
+        if planes > 1:
+
+            @pl.when(jnp.logical_and(outer, n == 0))
+            def _():
+                pl.semaphore_wait(relay.at[1], 1)
+
+            @pl.when(jnp.logical_and(outer, n == groups1 // planes))
+            def _():
+                pl.semaphore_wait(relay.at[2], 1)
+
         for d in range(per1):
             dest = g * per1 + d
 
@@ -186,7 +227,7 @@
         @pl.loop(0, groups1)
         def _(n):
             for d in range(per1):
-                dest = order(n, own1, groups1) * per1 + d
+                dest = order(n, own1, groups1, 1) * per1 + d
 
                 @pl.when(dest != me)
                 def _():
@@ -354,6 +395,7 @@
             sem((planes,)),
             sem,
             sem,
+            pltpu.SemaphoreType.REGULAR((3,)),
         ],
         compiler_params=pltpu.CompilerParams(collective_id=0, has_side_effects=True, vmem_limit_bytes=50 * 2**20),
         name="exchange",

time: 60.8 us -> 59.8 us (0.984)
  Pallas kernels: 59.9 us -> 58.9 us
    pallas_call x1, Pallas kernels: 58.2 us -> 57.2 us  [per_device(): pl.pallas_call(functools.partial(exchange_kernel, panels), out_shape=(jax...]
where the time goes in v2:
time: 59.8 us; the launch traced here: 59.6 us
  Pallas kernels  58.9 us (98%)
  between operations  0.64 us (1%)
    pallas_call x1, Pallas kernels, per_device(): pl.pallas_call(functools.partial(exchange_kernel, panels), out_shape=(jax...  57.2 us
    pallas_call x1, Pallas kernels, per_device(): pl.pallas_call(subtract_kernel, out_shape=(jax.ShapeDtypeStruct(recorded....  1.7 us

profile of v2, /device:TPU:0, one launch (start us, length us, event | category | flops | bytes accessed | tf_op | source)
XLA Modules:
  0.0 59.6 jit_solution(3646483222925317901)
XLA Ops:
  0.6 57.2 %exchange.1 = (f32[1,2,128,2048]{3,2,1,0:T(8,128)S(1)}, bf16[1,2,128,2048]{3,2,1,0:T(8,128)(2,1)S(1)}, f32[8,128]{1,0:T(8,128)S(1)}) custom-call(f32[1,2,128,2048]{3,2,1,0:T(8,128)} %rec_hbm.1, bf16[1,2,4095]{2,1,0:T(2,128)(2,1)} %rtaps_hbm.1, bf16[1,2,4095]{2,1,0:T(2,128)(2,1)} %staps_hbm.1), custom_call_target="tpu_custom_call" | custom-call | tf_op jit(solution)/shard_map/exchange/pallas_call | solution.py:368
  57.9 1.7 %subtract.1 = (f32[1,2,128,2048]{3,2,1,0:T(8,128)}, bf16[1,2,128,2048]{3,2,1,0:T(8,128)(2,1)}) custom-call(f32[1,2,128,2048]{3,2,1,0:T(8,128)S(1)} %get-tuple-element.5.rec_ref, bf16[1,2,128,2048]{3,2,1,0:T(8,128)(2,1)S(1)} %get-tuple-element.6.mult_ref, f32[8,128]{1,0:T(8,128)S(1)} %get-tuple-element.7.fit_ref), custom_call_target="tpu_custom_call" | custom-call | tf_op jit(solution)/shard_map/subtract/pallas_call | solution.py:405

commit v3 on v2

--- a/solution.py
+++ b/solution.py
@@ -13,6 +13,10 @@
 STRIP = 16
 STRIPS = 4
 PLANES = 4
+INNER1 = True
+CROSS1 = 1
+INNER2 = False
+CROSS2 = 1
 
 
 def spread(taps_ref, padded, comp, flipped):
@@ -35,14 +39,12 @@
     row = lax.broadcasted_iota(jnp.int32, (STRIP, length), 0)
     for comp in range(2):
         x = spread(taps_ref, padded, comp, flipped)
-        step = 1
-        while step < STRIP:
-            x = jnp.where((row & step) != 0, pltpu.roll(x, step, 1), x)
-            step *= 2
+        x = pltpu.roll(x, 0, 1, stride=1, stride_axis=0)
         lane0 = comp * block
+        xb = x.astype(jnp.bfloat16)
         for s in range(0, LANES, STRIP):
             shift = (s - (LANES - block) + (0 if flipped else 1)) % length
-            y = (pltpu.roll(x, shift, 1) if shift else x).astype(jnp.bfloat16)
+            y = jnp.concatenate([xb[:, length - shift :], xb[:, : length - shift]], axis=1) if shift else xb
             for m in range(length // LANES):
                 at = length - LANES * (m + 1)
                 band_ref[m * LANES + s : m * LANES + s + STRIP, lane0 : lane0 + block] = y[:, at : at + block]
@@ -50,6 +52,7 @@
 
 def exchange_kernel(
     panels,
+    planes,
     rec_hbm,
     rtaps_hbm,
     staps_hbm,
@@ -84,16 +87,19 @@
     cols = width // panels
     halves, hc = foc_in.shape[0], foc_in.shape[2]
     nt = (((1,), (1,)), ((), ()))
-    planes = recv2.shape[0]
     side = panels // planes
     plane = me // side
 
-    def order(n, own, groups, rev=0):
-        half = groups // 2
-        far = lax.rem(own // half + 1 + n // half, 2)
-        at = lax.rem(n, half)
-        at = jnp.where(far == 1 - rev, half - 1 - at, at)
-        return far * half + at + jnp.where(lax.rem(at, 2) == 0, 1, -1) * lax.rem(own, 2)
+    def order(n, own, groups, inner_first, cross):
+        wide = groups // planes
+        high = own // wide >= planes // 2
+        m = n // wide
+        if inner_first:
+            q = jnp.where(m < planes // 2, planes // 2 + m, planes - 1 - m)
+        else:
+            q = jnp.where(m < planes // 2, planes - 1 - m, m - planes // 2)
+        q = jnp.where(high, planes - 1 - q, q)
+        return q * wide + lax.rem(lax.rem(own, wide) + cross + n, wide)
 
     def peer(o):
         return lax.rem(me + o, panels)
@@ -104,16 +110,14 @@
             ((rtaps_hbm, rtaps_ref), (rec_hbm, rec_ref), (staps_hbm, staps_ref))
         )
     ]
-    for load in loads:
+    for load in loads[:2]:
         load.start()
 
     barrier = pltpu.get_barrier_semaphore()
 
-    @pl.loop(0, panels)
+    @pl.loop(jnp.maximum(plane - 1, 0) * side, jnp.minimum(plane + 2, planes) * side)
     def _(o):
-        gap = jnp.abs(o // side - plane)
-
-        @pl.when(jnp.logical_and(gap <= 1, o != me))
+        @pl.when(o != me)
         def _():
             pl.semaphore_signal(barrier, inc=1, device_id={"panel": o}, device_id_type=MESH)
 
@@ -130,15 +134,10 @@
 
     loads[0].wait()
     skew(rtaps_ref, padded, True, LANES, band_r)
+    loads[2].start()
     loads[1].wait()
-    for kb in range(width // LANES):
-        re = rec_ref[0, 0, :, kb * LANES : (kb + 1) * LANES].astype(jnp.bfloat16)
-        im = rec_ref[0, 1, :, kb * LANES : (kb + 1) * LANES].astype(jnp.bfloat16)
-        at = 2 * kb * LANES
-        w1[0:rows, at : at + LANES] = re
-        w1[0:rows, at + LANES : at + 2 * LANES] = -im
-        w1[rows : 2 * rows, at : at + LANES] = im
-        w1[rows : 2 * rows, at + LANES : at + 2 * LANES] = re
+    for comp in range(2):
+        w1[comp * rows : (comp + 1) * rows, :] = rec_ref[0, comp].astype(jnp.bfloat16)
 
     pl.semaphore_wait(barrier, side * (1 + above + below) - 1)
     if planes > 1:
@@ -163,7 +162,7 @@
             src_ref=mul.at[h, pl.ds(pl.multiple_of(dest * rows, rows), rows), :],
             dst_ref=mul_in.at[h, src],
             send_sem=send2,
-            recv_sem=recv2.at[src // side],
+            recv_sem=recv2.at[src // per2],
             device_id={"panel": dest},
             device_id_type=MESH,
         )
@@ -187,7 +186,7 @@
 
     @pl.loop(0, groups1)
     def _(n):
-        g = order(n, own1, groups1, 1)
+        g = order(n, own1, groups1, INNER1, CROSS1)
         if planes > 1:
 
             @pl.when(jnp.logical_and(inner, n == groups1 // planes))
@@ -196,14 +195,21 @@
                 tell(2, outward)
 
         first = pl.multiple_of(g * GROUP, GROUP)
-        lhs = jnp.concatenate(
-            [
-                band_r[pl.ds(pl.multiple_of(width - LANES * (kb + 1) + first, LANES), GROUP), :]
-                for kb in range(width // LANES)
-            ],
-            axis=1,
-        )
-        out = lax.dot_general(lhs, w1[...], nt, preferred_element_type=jnp.float32)
+        parts = []
+        for comp in range(2):
+            lhs = jnp.concatenate(
+                [
+                    band_r[
+                        pl.ds(pl.multiple_of(width - LANES * (kb + 1) + first, LANES), GROUP),
+                        comp * LANES : (comp + 1) * LANES,
+                    ]
+                    for kb in range(width // LANES)
+                ],
+                axis=1,
+            )
+            parts.append(lax.dot_general(lhs, w1[...], nt, preferred_element_type=jnp.float32))
+        re, im = parts
+        out = jnp.concatenate([re[:, :rows] - im[:, rows:], re[:, rows:] + im[:, :rows]], axis=1)
         foc[pl.ds(first, GROUP), :] = out.astype(jnp.bfloat16)
         if planes > 1:
 
@@ -227,7 +233,7 @@
         @pl.loop(0, groups1)
         def _(n):
             for d in range(per1):
-                dest = order(n, own1, groups1, 1) * per1 + d
+                dest = order(n, own1, groups1, INNER1, CROSS1) * per1 + d
 
                 @pl.when(dest != me)
                 def _():
@@ -252,7 +258,7 @@
 
         @pl.loop(0, groups2)
         def _(n):
-            g = order(n, own2, groups2)
+            g = order(n, own2, groups2, INNER2, CROSS2)
             first = pl.multiple_of(g * GROUP, GROUP)
             lhs = jnp.concatenate(
                 [
@@ -276,11 +282,11 @@
         return jnp.sum(v, axis=0, keepdims=True)
 
     near = LANES // cols
-    chunks = side // near
+    chunks = per2 // near
 
     def gather(q, count, acc):
         if count:
-            drain(mul_in.at[:, pl.ds(q * side, count)], recv2.at[q])
+            drain(mul_in.at[:, pl.ds(q * per2, count)], recv2.at[q])
 
         def step(n, acc):
             cb = q * chunks + n
@@ -303,14 +309,18 @@
         return lax.fori_loop(0, chunks, step, acc)
 
     zero = jnp.zeros((1, LANES), jnp.float32)
-    sides = gather(plane, side - 1, (zero, zero, zero))
+    wide = groups2 // planes
+    place = own2 - plane * wide
 
     def visit(n, acc):
+        m = n // wide
         p = jnp.where(plane < planes // 2, plane, planes - 1 - plane)
-        q = jnp.where(n < planes // 2 - 1, n + (n >= p), planes + planes // 2 - 2 - n)
-        return gather(jnp.where(plane < planes // 2, q, planes - 1 - q), side, acc)
-
-    num_re, num_im, energy = lax.fori_loop(0, planes - 1, visit, sides)
+        q = jnp.where(m == 0, p, jnp.where(m < planes // 2, m - (m <= p), planes + planes // 2 - 1 - m))
+        q = jnp.where(plane < planes // 2, q, planes - 1 - q)
+        at = lax.rem(n, wide)
+        return gather(q * wide + jnp.where(m == 0, lax.rem(place + at, wide), lax.rem(place + 1 + at, wide)), per2, acc)
+
+    num_re, num_im, energy = lax.fori_loop(1, groups2, visit, gather(own2, per2 - 1, (zero, zero, zero)))
     part = jnp.concatenate([num_re, num_im, energy, jnp.zeros((5, LANES), jnp.float32)], axis=0)
     sums[...] = part
     sums_in[me] = part
@@ -362,11 +372,11 @@
     vmem = pl.BlockSpec(memory_space=pltpu.VMEM)
     hc = min(cols, LANES // 2)
     halves = cols // hc
-    planes = PLANES if panels % PLANES == 0 else 1
+    planes = PLANES if (width // GROUP) % PLANES == 0 and (sources // GROUP) % PLANES == 0 else 1
     sem = pltpu.SemaphoreType.DMA
     hbm = pl.BlockSpec(memory_space=pltpu.HBM)
     rec, mult, fit = pl.pallas_call(
-        functools.partial(exchange_kernel, panels),
+        functools.partial(exchange_kernel, panels, planes),
         out_shape=(
             jax.ShapeDtypeStruct(recorded.shape, jnp.float32),
             jax.ShapeDtypeStruct(recorded.shape, bf16),
@@ -381,7 +391,7 @@
             pltpu.VMEM((2, 2 * width), jnp.float32),
             pltpu.VMEM((2 * width, 2 * LANES), bf16),
             pltpu.VMEM((2 * sources, 2 * rows), bf16),
-            pltpu.VMEM((2 * rows, 2 * width), bf16),
+            pltpu.VMEM((2 * rows, width), bf16),
             pltpu.VMEM((2 * hc, 2 * sources), bf16),
             pltpu.VMEM((width, 2 * rows), bf16),
             pltpu.VMEM((halves, panels, hc, 2 * rows), bf16),
@@ -392,7 +402,7 @@
             sem,
             sem((halves,)),
             sem,
-            sem((planes,)),
+            sem((sources // GROUP,)),
             sem,
             sem,
             pltpu.SemaphoreType.REGULAR((3,)),

time: 59.8 us -> 58.7 us (0.982)
  Pallas kernels: 58.9 us -> 57.8 us
    pallas_call x1, Pallas kernels: 57.2 us -> 56.1 us  [per_device(): pl.pallas_call(functools.partial(exchange_kernel, panels, planes), out_sh...]
where the time goes in v3:
time: 58.7 us; the launch traced here: 58.5 us
  Pallas kernels  57.8 us (98%)
  between operations  0.64 us (1%)
    pallas_call x1, Pallas kernels, per_device(): pl.pallas_call(functools.partial(exchange_kernel, panels, planes), out_sh...  56.1 us
    pallas_call x1, Pallas kernels, per_device(): pl.pallas_call(subtract_kernel, out_shape=(jax.ShapeDtypeStruct(recorded....  1.7 us

profile of v3, /device:TPU:0, one launch (start us, length us, event | category | flops | bytes accessed | tf_op | source)
XLA Modules:
  0.0 58.5 jit_solution(1226511910025612741)
XLA Ops:
  0.6 56.1 %exchange.1 = (f32[1,2,128,2048]{3,2,1,0:T(8,128)S(1)}, bf16[1,2,128,2048]{3,2,1,0:T(8,128)(2,1)S(1)}, f32[8,128]{1,0:T(8,128)S(1)}) custom-call(f32[1,2,128,2048]{3,2,1,0:T(8,128)} %rec_hbm.1, bf16[1,2,4095]{2,1,0:T(2,128)(2,1)} %rtaps_hbm.1, bf16[1,2,4095]{2,1,0:T(2,128)(2,1)} %staps_hbm.1), custom_call_target="tpu_custom_call" | custom-call | tf_op jit(solution)/shard_map/exchange/pallas_call | solution.py:378
  56.8 1.7 %subtract.1 = (f32[1,2,128,2048]{3,2,1,0:T(8,128)}, bf16[1,2,128,2048]{3,2,1,0:T(8,128)(2,1)}) custom-call(f32[1,2,128,2048]{3,2,1,0:T(8,128)S(1)} %get-tuple-element.5.rec_ref, bf16[1,2,128,2048]{3,2,1,0:T(8,128)(2,1)S(1)} %get-tuple-element.6.mult_ref, f32[8,128]{1,0:T(8,128)S(1)} %get-tuple-element.7.fit_ref), custom_call_target="tpu_custom_call" | custom-call | tf_op jit(solution)/shard_map/subtract/pallas_call | solution.py:415

commit v4 on v3

--- a/solution.py
+++ b/solution.py
@@ -11,10 +11,11 @@
 LANES = 128
 GROUP = 256
 STRIP = 16
+SUBLANES = 8
 STRIPS = 4
 PLANES = 4
 INNER1 = True
-CROSS1 = 1
+CROSS1 = 0
 INNER2 = False
 CROSS2 = 1
 
@@ -27,9 +28,10 @@
     i = lax.broadcasted_iota(jnp.int32, (LANES, LANES), 0)
     j = lax.broadcasted_iota(jnp.int32, (LANES, LANES), 1)
     swap = jnp.where(i + j == LANES - 1, 1.0, 0.0).astype(jnp.bfloat16)
-    tall = jnp.concatenate([jnp.broadcast_to(r, (STRIP, LANES)) for r in rows[::-1]], axis=0)
+    tall = jnp.concatenate([jnp.broadcast_to(r, (SUBLANES, LANES)) for r in rows[::-1]], axis=0)
     tall = jnp.dot(tall.astype(jnp.bfloat16), swap, preferred_element_type=jnp.float32)
-    return jnp.concatenate([tall[at : at + STRIP] for at in range(0, tall.shape[0], STRIP)], axis=1)
+    x = jnp.concatenate([tall[at : at + SUBLANES] for at in range(0, tall.shape[0], SUBLANES)], axis=1)
+    return jnp.concatenate([x] * (STRIP // SUBLANES), axis=0)
 
 
 def skew(taps_ref, padded, flipped, block, band_ref):
@@ -115,14 +117,30 @@
 
     barrier = pltpu.get_barrier_semaphore()
 
-    @pl.loop(jnp.maximum(plane - 1, 0) * side, jnp.minimum(plane + 2, planes) * side)
-    def _(o):
-        @pl.when(o != me)
-        def _():
-            pl.semaphore_signal(barrier, inc=1, device_id={"panel": o}, device_id_type=MESH)
-
     above = (plane > 0).astype(jnp.int32)
     below = (plane < planes - 1).astype(jnp.int32)
+    groups1 = width // GROUP
+    per1 = GROUP // cols
+    own1 = me // per1
+    wide1 = groups1 // planes
+
+    def greet(o):
+        pl.semaphore_signal(barrier, inc=1, device_id={"panel": o}, device_id_type=MESH)
+
+    for d in range(per1):
+
+        @pl.when(plane > 0)
+        def _():
+            greet(own1 * per1 - side + d)
+
+        @pl.when(plane < planes - 1)
+        def _():
+            greet(own1 * per1 + side + d)
+
+    @pl.loop(1, side)
+    def _(o):
+        greet(plane * side + lax.rem(me - plane * side + o, side))
+
 
     outer = jnp.logical_or(plane == 0, plane == planes - 1)
     inner = jnp.logical_not(outer)
@@ -139,13 +157,10 @@
     for comp in range(2):
         w1[comp * rows : (comp + 1) * rows, :] = rec_ref[0, comp].astype(jnp.bfloat16)
 
-    pl.semaphore_wait(barrier, side * (1 + above + below) - 1)
-    if planes > 1:
-
-        @pl.when(inner)
-        def _():
-            tell(0, inward)
-            tell(1, outward)
+    pl.semaphore_wait(barrier, side - 1 + per1 * (above + below))
+    for k in range(1, wide1):
+        dest = plane * side + lax.rem(me - plane * side + k * per1, side)
+        pl.semaphore_signal(relay.at[3], inc=1, device_id={"panel": dest}, device_id_type=MESH)
 
     def copy1(h, dest, src):
         return pltpu.make_async_remote_copy(
@@ -179,10 +194,6 @@
             device_id={"panel": dest},
             device_id_type=MESH,
         )
-
-    groups1 = width // GROUP
-    per1 = GROUP // cols
-    own1 = me // per1
 
     @pl.loop(0, groups1)
     def _(n):
@@ -228,6 +239,17 @@
             def _():
                 copy1(0, dest, me).start()
 
+        @pl.when(n == 0)
+        def _():
+            if wide1 > 1:
+                pl.semaphore_wait(relay.at[3], wide1 - 1)
+            if planes > 1:
+
+                @pl.when(inner)
+                def _():
+                    tell(0, inward)
+                    tell(1, outward)
+
     for h in range(1, halves):
 
         @pl.loop(0, groups1)
@@ -279,7 +301,7 @@
         mul_in[h, me] = mul[h, pl.ds(pl.multiple_of(me * rows, rows), rows), :]
 
     def fold(v):
-        return jnp.sum(v, axis=0, keepdims=True)
+        return jnp.sum(v.reshape(rows // SUBLANES, SUBLANES, LANES), axis=0)
 
     near = LANES // cols
     chunks = per2 // near
@@ -308,7 +330,7 @@
 
         return lax.fori_loop(0, chunks, step, acc)
 
-    zero = jnp.zeros((1, LANES), jnp.float32)
+    zero = jnp.zeros((SUBLANES, LANES), jnp.float32)
     wide = groups2 // planes
     place = own2 - plane * wide
 
@@ -321,7 +343,9 @@
         return gather(q * wide + jnp.where(m == 0, lax.rem(place + at, wide), lax.rem(place + 1 + at, wide)), per2, acc)
 
     num_re, num_im, energy = lax.fori_loop(1, groups2, visit, gather(own2, per2 - 1, (zero, zero, zero)))
-    part = jnp.concatenate([num_re, num_im, energy, jnp.zeros((5, LANES), jnp.float32)], axis=0)
+    sub = lax.broadcasted_iota(jnp.int32, (SUBLANES, LANES), 0)
+    num_re, num_im, energy = (jnp.sum(v, axis=0, keepdims=True) for v in (num_re, num_im, energy))
+    part = jnp.where(sub == 0, num_re, jnp.where(sub == 1, num_im, jnp.where(sub == 2, energy, 0.0)))
     sums[...] = part
     sums_in[me] = part
 
@@ -405,7 +429,7 @@
             sem((sources // GROUP,)),
             sem,
             sem,
-            pltpu.SemaphoreType.REGULAR((3,)),
+            pltpu.SemaphoreType.REGULAR((4,)),
         ],
         compiler_params=pltpu.CompilerParams(collective_id=0, has_side_effects=True, vmem_limit_bytes=50 * 2**20),
         name="exchange",

time: 58.7 us -> 58.6 us (level)
  no operation moved by 1% of the time
where the time goes in v4:
time: 58.6 us; the launch traced here: 58.4 us
  Pallas kernels  57.7 us (98%)
  between operations  0.64 us (1%)
    pallas_call x1, Pallas kernels, per_device(): pl.pallas_call(functools.partial(exchange_kernel, panels, planes), out_sh...  56 us
    pallas_call x1, Pallas kernels, per_device(): pl.pallas_call(subtract_kernel, out_shape=(jax.ShapeDtypeStruct(recorded....  1.7 us

profile of v4, /device:TPU:0, one launch (start us, length us, event | category | flops | bytes accessed | tf_op | source)
XLA Modules:
  0.0 58.4 jit_solution(1863431552703211700)
XLA Ops:
  0.6 56.0 %exchange.1 = (f32[1,2,128,2048]{3,2,1,0:T(8,128)S(1)}, bf16[1,2,128,2048]{3,2,1,0:T(8,128)(2,1)S(1)}, f32[8,128]{1,0:T(8,128)S(1)}) custom-call(f32[1,2,128,2048]{3,2,1,0:T(8,128)} %rec_hbm.1, bf16[1,2,4095]{2,1,0:T(2,128)(2,1)} %rtaps_hbm.1, bf16[1,2,4095]{2,1,0:T(2,128)(2,1)} %staps_hbm.1), custom_call_target="tpu_custom_call" | custom-call | tf_op jit(solution)/shard_map/exchange/pallas_call | solution.py:402
  56.7 1.7 %subtract.1 = (f32[1,2,128,2048]{3,2,1,0:T(8,128)}, bf16[1,2,128,2048]{3,2,1,0:T(8,128)(2,1)}) custom-call(f32[1,2,128,2048]{3,2,1,0:T(8,128)S(1)} %get-tuple-element.5.rec_ref, bf16[1,2,128,2048]{3,2,1,0:T(8,128)(2,1)S(1)} %get-tuple-element.6.mult_ref, f32[8,128]{1,0:T(8,128)S(1)} %get-tuple-element.7.fit_ref), custom_call_target="tpu_custom_call" | custom-call | tf_op jit(solution)/shard_map/subtract/pallas_call | solution.py:439

commit v5 on v4

--- a/solution.py
+++ b/solution.py
@@ -349,27 +349,26 @@
     sums[...] = part
     sums_in[me] = part
 
-    @pl.loop(1, panels)
+    @pl.loop(0, panels)
     def _(o):
-        copy3(peer(o), me).start()
+        @pl.when(o != me)
+        def _():
+            copy3(o, me).start()
 
     drain(foc.at[pl.ds(0, width - cols), :], send1)
     drain(mul.at[:, pl.ds(0, sources - rows), :], send2)
     drain(sums_in.at[pl.ds(0, panels - 1)], recv3)
     drain(sums_in.at[pl.ds(0, panels - 1)], send3)
 
-    total = jnp.sum(jnp.sum(sums_in[...], axis=0), axis=1, keepdims=True)
-    fit = total[0:2, :] / (total[2:3, :] + 1e-06)
-    fit_ref[...] = jnp.broadcast_to(
-        jnp.concatenate([fit, jnp.zeros((6, 1), jnp.float32)], axis=0), (8, LANES)
-    )
+    fit_ref[...] = jnp.sum(sums_in[...], axis=0)
 
 
 def subtract_kernel(rec_ref, mult_ref, fit_ref, prim_hbm, mult_hbm, prim, sem):
     mult_out = pltpu.make_async_copy(mult_ref, mult_hbm, sem.at[0])
     mult_out.start()
-    fit_re = fit_ref[0:1, 0:1]
-    fit_im = fit_ref[1:2, 0:1]
+    total = jnp.sum(fit_ref[...], axis=1, keepdims=True)
+    fit_re = total[0:1, :] / (total[2:3, :] + 1e-06)
+    fit_im = total[1:2, :] / (total[2:3, :] + 1e-06)
     rows = rec_ref.shape[2]
     strip = rows // STRIPS
     outs = []

time: 58.6 us -> 58.3 us (level)
  no operation moved by 1% of the time
where the time goes in v5:
time: 58.3 us; the launch traced here: 58.1 us
  Pallas kernels  57.4 us (98%)
  between operations  0.64 us (1%)
    pallas_call x1, Pallas kernels, per_device(): pl.pallas_call(functools.partial(exchange_kernel, panels, planes), out_sh...  55.7 us
    pallas_call x1, Pallas kernels, per_device(): pl.pallas_call(subtract_kernel, out_shape=(jax.ShapeDtypeStruct(recorded....  1.7 us

profile of v5, /device:TPU:0, one launch (start us, length us, event | category | flops | bytes accessed | tf_op | source)
XLA Modules:
  0.0 58.1 jit_solution(13978083784016003719)
XLA Ops:
  0.6 55.7 %exchange.1 = (f32[1,2,128,2048]{3,2,1,0:T(8,128)S(1)}, bf16[1,2,128,2048]{3,2,1,0:T(8,128)(2,1)S(1)}, f32[8,128]{1,0:T(8,128)S(1)}) custom-call(f32[1,2,128,2048]{3,2,1,0:T(8,128)} %rec_hbm.1, bf16[1,2,4095]{2,1,0:T(2,128)(2,1)} %rtaps_hbm.1, bf16[1,2,4095]{2,1,0:T(2,128)(2,1)} %staps_hbm.1), custom_call_target="tpu_custom_call" | custom-call | tf_op jit(solution)/shard_map/exchange/pallas_call | solution.py:401
  56.4 1.7 %subtract.1 = (f32[1,2,128,2048]{3,2,1,0:T(8,128)}, bf16[1,2,128,2048]{3,2,1,0:T(8,128)(2,1)}) custom-call(f32[1,2,128,2048]{3,2,1,0:T(8,128)S(1)} %get-tuple-element.5.rec_ref, bf16[1,2,128,2048]{3,2,1,0:T(8,128)(2,1)S(1)} %get-tuple-element.6.mult_ref, f32[8,128]{1,0:T(8,128)S(1)} %get-tuple-element.7.fit_ref), custom_call_target="tpu_custom_call" | custom-call | tf_op jit(solution)/shard_map/subtract/pallas_call | solution.py:438

commit v6 on v5

--- a/solution.py
+++ b/solution.py
@@ -101,7 +101,8 @@
         else:
             q = jnp.where(m < planes // 2, planes - 1 - m, m - planes // 2)
         q = jnp.where(high, planes - 1 - q, q)
-        return q * wide + lax.rem(lax.rem(own, wide) + cross + n, wide)
+        turn = jnp.where(m == planes // 2 - 1, cross, 0)
+        return q * wide + lax.rem(lax.rem(own, wide) + turn + n, wide)
 
     def peer(o):
         return lax.rem(me + o, panels)

time: 58.3 us -> 58.3 us (level)
  no operation moved by 1% of the time
where the time goes in v6:
time: 58.3 us; the launch traced here: 58.1 us
  Pallas kernels  57.4 us (98%)
  between operations  0.64 us (1%)
    pallas_call x1, Pallas kernels, per_device(): pl.pallas_call(functools.partial(exchange_kernel, panels, planes), out_sh...  55.7 us
    pallas_call x1, Pallas kernels, per_device(): pl.pallas_call(subtract_kernel, out_shape=(jax.ShapeDtypeStruct(recorded....  1.7 us

profile of v6, /device:TPU:0, one launch (start us, length us, event | category | flops | bytes accessed | tf_op | source)
XLA Modules:
  0.0 58.1 jit_solution(42157319608198898)
XLA Ops:
  0.6 55.7 %exchange.1 = (f32[1,2,128,2048]{3,2,1,0:T(8,128)S(1)}, bf16[1,2,128,2048]{3,2,1,0:T(8,128)(2,1)S(1)}, f32[8,128]{1,0:T(8,128)S(1)}) custom-call(f32[1,2,128,2048]{3,2,1,0:T(8,128)} %rec_hbm.1, bf16[1,2,4095]{2,1,0:T(2,128)(2,1)} %rtaps_hbm.1, bf16[1,2,4095]{2,1,0:T(2,128)(2,1)} %staps_hbm.1), custom_call_target="tpu_custom_call" | custom-call | tf_op jit(solution)/shard_map/exchange/pallas_call | solution.py:402
  56.4 1.7 %subtract.1 = (f32[1,2,128,2048]{3,2,1,0:T(8,128)}, bf16[1,2,128,2048]{3,2,1,0:T(8,128)(2,1)}) custom-call(f32[1,2,128,2048]{3,2,1,0:T(8,128)S(1)} %get-tuple-element.5.rec_ref, bf16[1,2,128,2048]{3,2,1,0:T(8,128)(2,1)S(1)} %get-tuple-element.6.mult_ref, f32[8,128]{1,0:T(8,128)S(1)} %get-tuple-element.7.fit_ref), custom_call_target="tpu_custom_call" | custom-call | tf_op jit(solution)/shard_map/subtract/pallas_call | solution.py:439

commit v7 on v6

--- a/solution.py
+++ b/solution.py
@@ -329,7 +329,7 @@
                 acc[2] + fold(mre * mre + mim * mim),
             )
 
-        return lax.fori_loop(0, chunks, step, acc)
+        return lax.fori_loop(0, chunks, step, acc, unroll=True)
 
     zero = jnp.zeros((SUBLANES, LANES), jnp.float32)
     wide = groups2 // planes

time: 58.3 us -> 58.3 us (level)
  no operation moved by 1% of the time
where the time goes in v7:
time: 58.3 us; the launch traced here: 58 us
  Pallas kernels  57.4 us (98%)
  between operations  0.64 us (1%)
    pallas_call x1, Pallas kernels, per_device(): pl.pallas_call(functools.partial(exchange_kernel, panels, planes), out_sh...  55.7 us
    pallas_call x1, Pallas kernels, per_device(): pl.pallas_call(subtract_kernel, out_shape=(jax.ShapeDtypeStruct(recorded....  1.7 us

profile of v7, /device:TPU:0, one launch (start us, length us, event | category | flops | bytes accessed | tf_op | source)
XLA Modules:
  0.0 58.0 jit_solution(2662974751275952755)
XLA Ops:
  0.6 55.7 %exchange.1 = (f32[1,2,128,2048]{3,2,1,0:T(8,128)S(1)}, bf16[1,2,128,2048]{3,2,1,0:T(8,128)(2,1)S(1)}, f32[8,128]{1,0:T(8,128)S(1)}) custom-call(f32[1,2,128,2048]{3,2,1,0:T(8,128)} %rec_hbm.1, bf16[1,2,4095]{2,1,0:T(2,128)(2,1)} %rtaps_hbm.1, bf16[1,2,4095]{2,1,0:T(2,128)(2,1)} %staps_hbm.1), custom_call_target="tpu_custom_call" | custom-call | tf_op jit(solution)/shard_map/exchange/pallas_call | solution.py:402
  56.3 1.7 %subtract.1 = (f32[1,2,128,2048]{3,2,1,0:T(8,128)}, bf16[1,2,128,2048]{3,2,1,0:T(8,128)(2,1)}) custom-call(f32[1,2,128,2048]{3,2,1,0:T(8,128)S(1)} %get-tuple-element.5.rec_ref, bf16[1,2,128,2048]{3,2,1,0:T(8,128)(2,1)S(1)} %get-tuple-element.6.mult_ref, f32[8,128]{1,0:T(8,128)S(1)} %get-tuple-element.7.fit_ref), custom_call_target="tpu_custom_call" | custom-call | tf_op jit(solution)/shard_map/subtract/pallas_call | solution.py:439
